TPU v7x, 512 devices: a whole 4x8x8 slice. The times are simulated.
512 devices in a mesh: gx: 8 (over x, y_hi), gy: 8 (over z), gz: 8 (over y_lo, core).
Axes of the slice: x: 4, y: 8 (y_hi: 2, y_lo: 4; y = y_hi * 4 + y_lo), z: 8, core: 2. Of those that a mesh axis runs over, the one named last changes fastest.
Arguments:
- correlators: bfloat16 [32, 64, 64, 64, 128], P(None, 'gx', 'gy', 'gz'), may hold values from -6 to 6
- momenta: int32 [125, 3], replicated, may hold values from -32 to 31
- source_channel: int32 [64], replicated, may hold values from 0 to 63
- phase_code: int32 [64], replicated, may hold values from 0 to 3
Outputs:
- projected: float32 [32, 125, 128], P('gx', None, ('gy', 'gz'))
All inputs are finite; a program needn't handle non-finite values.
Results may differ from a plain program's by a relative error of at most 0.002.
Values sent between devices are 32-bit elements; how exact they have to be, the bound alone decides.
A program may use at most 64 MiB of HBM per device.

v0:
```python
import math

import jax
import jax.numpy as jnp
from jax import lax
from jax.sharding import Mesh
from jax.sharding import PartitionSpec as P

GZ = ("gz_0", "gz_1")
GY_GZ = ("gy", "gz_0", "gz_1")


def in_blocks(value, dim, size):
    lengths = value.shape
    blocks = value.reshape(*lengths[:dim], size, lengths[dim] // size, *lengths[dim + 1 :])
    return jnp.moveaxis(blocks, dim, 0)


def summed_on_arrival(value, axis, dim):
    blocks = in_blocks(value, dim, lax.axis_size(axis))
    arrived = lax.all_to_all(blocks, axis, split_axis=0, concat_axis=0, tiled=True)
    return arrived.sum(axis=0)


def sum_by_axis(value, axes, dim):
    far, near = axes
    own = summed_on_arrival(in_blocks(value, dim, lax.axis_size(far)), near, dim + 1)
    return jnp.sum(lax.all_to_all(own, far, 0, 0, tiled=True), axis=0)


def axis_fraction(values, coords, extent):
    return jnp.mod(values[:, None] * coords[None, :], extent).astype(jnp.float32) / extent


def phase_table(momenta, coord_x, coord_y, coord_z, size_x, size_y, size_z):
    frac_x = axis_fraction(momenta[:, 0], coord_x, size_x)
    frac_y = axis_fraction(momenta[:, 1], coord_y, size_y)
    frac_z = axis_fraction(momenta[:, 2], coord_z, size_z)
    summed = frac_x[:, :, None, None] + frac_y[:, None, :, None]
    summed = summed + frac_z[:, None, None, :]
    angles = (summed * (2.0 * math.pi)).reshape(momenta.shape[0], -1)
    return jnp.concatenate([jnp.cos(angles), jnp.sin(angles)], axis=0).astype(jnp.bfloat16)


def channel_signs(phase_code):
    real_sign = jnp.where(phase_code == 0, 1.0, jnp.where(phase_code == 2, -1.0, 0.0)).astype(
        jnp.float32
    )
    imag_sign = jnp.where(phase_code == 1, 1.0, jnp.where(phase_code == 3, -1.0, 0.0)).astype(
        jnp.float32
    )
    return (real_sign, imag_sign)


def local(correlators, momenta, source_channel, phase_code):
    window, cells_x, cells_y, cells_z, width = correlators.shape
    channels = width // 2
    moment_count = momenta.shape[0]
    size_x = cells_x * lax.axis_size("gx")
    size_y = cells_y * lax.axis_size("gy")
    size_z = cells_z * lax.axis_size(GZ)
    coord_x = lax.axis_index("gx") * cells_x + jnp.arange(cells_x, dtype=jnp.int32)
    coord_y = lax.axis_index("gy") * cells_y + jnp.arange(cells_y, dtype=jnp.int32)
    coord_z = lax.axis_index(GZ) * cells_z + jnp.arange(cells_z, dtype=jnp.int32)
    phases = phase_table(momenta, coord_x, coord_y, coord_z, size_x, size_y, size_z)
    real_sign, imag_sign = channel_signs(phase_code)
    chosen = (jnp.arange(channels, dtype=jnp.int32)[:, None] == source_channel[None, :]).astype(
        jnp.float32
    )
    from_real = jnp.concatenate([chosen * real_sign[None, :], chosen * imag_sign[None, :]], axis=1)
    from_imag = jnp.concatenate([-chosen * imag_sign[None, :], chosen * real_sign[None, :]], axis=1)
    mixing = jnp.concatenate([from_real, from_imag], axis=0).astype(jnp.bfloat16)
    site_count = cells_x * cells_y * cells_z
    flat = correlators.reshape(window, site_count, width)
    norm_factor = 1.0 / math.sqrt(size_x * size_y * size_z)
    mixed = jnp.dot(flat.reshape(-1, width), mixing, preferred_element_type=jnp.float32)
    mixed = mixed.astype(jnp.bfloat16).reshape(window, site_count, width)
    product = jnp.einsum("ms,tsc->tmc", phases, mixed, preferred_element_type=jnp.float32)
    cos_part = product[:, :moment_count]
    sin_part = product[:, moment_count:]
    real_out = cos_part[:, :, :channels] + sin_part[:, :, channels:]
    imag_out = cos_part[:, :, channels:] - sin_part[:, :, :channels]
    partial_value = jnp.concatenate([real_out, imag_out], axis=2) * norm_factor
    summed = sum_by_axis(partial_value, (("gy", "gz_0"), "gz_1"), 2)
    return summed_on_arrival(summed, "gx", 0)


def solution(mesh):
    split = Mesh(
        mesh.devices.reshape(mesh.shape["gx"], mesh.shape["gy"], 4, 2), ("gx", "gy", "gz_0", "gz_1")
    )
    return jax.shard_map(
        local,
        mesh=split,
        in_specs=(P(None, "gx", "gy", GZ, None), P(), P(), P()),
        out_specs=P("gx", None, GY_GZ),
        check_vma=False,
    )
```

profile of v0, /device:TPU:16, one launch (start us, length us, event | category | flops | bytes accessed | tf_op | source)
XLA Modules:
  0.0 81.6 jit_solution(5675193427421453078)
XLA Ops:
  0.0 0.7 compare_select_fusion.1
  0.7 0.7 compare_select_fusion.3
  1.3 0.8 slice_bitcast_fusion.2
  2.1 0.7 multiply_convert_fusion
  2.8 0.7 select_convert_fusion
  3.5 0.1 fusion.20
  3.6 0.1 fusion.16
  3.6 1.0 %cosine_convert_fusion = (bf16[125,8,8,8]{0,3,2,1:T(8,128)(2,1)S(1)}, bf16[125,8,8,8]{0,3,2,1:T(8,128)(2,1)S(1)}) fusion(f32[125,8]{0,1:T(8,128)S(1)} %fusion.20, f32[125,8,8]{0,2,1:T(8,128)S(1)} %broadcast_add_fusion), kind=kLoop, calls=%fused_computation.12 | loop fusion | flops 256000 | bytes 292000 | tf_op jit(solution)/shard_map/convert.3
  4.7 0.1 copy.23
  4.8 0.1 copy.24
  4.9 3.5 %convolution_convert_fusion = bf16[128,16384]{1,0:T(8,128)(2,1)S(1)} fusion(bf16[16384,128]{1,0:T(8,128)(2,1)} %bitcast.32, bf16[64,64]{1,0:T(8,128)(2,1)S(1)} %get-tuple-element.13, bf16[64,64]{1,0:T(8,128)(2,1)S(1)} %multiply_convert_fusion, bf16[64,64]{1,0:T(8,128)(2,1)S(1)} %get-tuple-element.12), kind=kOutput, calls=%fused_computation | convolution fusion | flops 539099136 | bytes 8413184 | tf_op jit(solution)/shard_map/dot_general | solution.py:76
  8.5 1.3 %fusion.3 = f32[32,250,128]{1,2,0:T(8,128)S(1)} fusion(bf16[16,32,8,512]{3,2,1,0:T(8,128)(2,1)S(1)} %bitcast.30, bf16[125,512]{1,0:T(8,128)(2,1)S(1)} %copy.24, bf16[125,512]{1,0:T(8,128)(2,1)S(1)} %copy.23), kind=kOutput, calls=%fused_computation.4 | convolution fusion | flops 1049088000 | bytes 8546304 | tf_op jit(solution)/shard_map/ms,tsc->tmc/dot_general | solution.py:78
  9.8 0.6 slice_add_fusion
  10.4 0.6 copy.26
  11.0 0.6 copy.27
  11.6 0.4 maximum_multiply_fusion
  12.0 1.6 %copy.28 = f32[2,32,32,125,2]{3,4,1,2,0:T(2,128)S(1)} copy(f32[2,32,32,125,2]{3,2,4,0,1:T(8,128)S(1)} %bitcast.31) | data formatting | bytes 4096000 | tf_op jit(solution)/shard_map/transpose | solution.py:16
  13.7 5.4 %all_to_all.15 = f32[2,32,32,125,2]{3,4,1,2,0:T(2,128)S(1)} all-to-all(f32[2,32,32,125,2]{3,4,1,2,0:T(2,128)S(1)} %copy.28), channel_id=1, replica_groups=mesh['gx'=8,'gy'=8,'gz_0'=4,'gz_1'=2] {'gz_1'}, dimensions={0} | all-to-all | bytes 4096000 | tf_op jit(solution)/shard_map/all_to_all | solution.py:21
  19.1 2.3 %reduce_sum.27 = f32[32,32,125,2]{2,3,0,1:T(2,128)S(1)} reduce(f32[2,32,32,125,2]{3,4,1,2,0:T(2,128)S(1)} %all_to_all.15, f32[]{:T(128)} %constant.55.clone.1), dimensions={0}, to_apply=%region_0.1 | reduce | flops 256000 | bytes 3072004 | tf_op jit(solution)/shard_map/reduce_sum | solution.py:22
  21.4 0.6 copy.30
  22.0 42.0 %all_to_all.16 = f32[32,32,125,2]{2,1,3,0:T(8,128)S(1)} all-to-all(f32[32,32,125,2]{2,1,3,0:T(8,128)S(1)} %copy.30), channel_id=1, replica_groups=mesh['gx'=8,'gy'=8,'gz_0'=4,'gz_1'=2] {'gy','gz_0'}, dimensions={0} | all-to-all | bytes 2048000 | tf_op jit(solution)/shard_map/all_to_all | solution.py:28
  64.0 0.1 reduce_sum.28
  64.1 16.8 %all_to_all.17 = f32[8,4,125,2]{2,1,3,0:T(4,128)S(1)} all-to-all(f32[8,4,125,2]{2,1,3,0:T(4,128)S(1)} %copy.31), channel_id=1, replica_groups=mesh['gx'=8,'gy'=8,'gz_0'=4,'gz_1'=2] {'gx'}, dimensions={0} | all-to-all | bytes 64000 | tf_op jit(solution)/shard_map/all_to_all | solution.py:21
  81.0 0.6 copy.32
  (6 shorter events, 0.0 us)
where the time goes:
time: 81.9 us; the launch traced here: 81.6 us
  blocking collectives  64.3 us (79%)
  other arithmetic  7.24 us (9%)
  local copies, waits for them, and re-layouts  5.14 us (6%)
  matrix products  4.84 us (6%)
    all_to_all x1, blocking collectives, sum_by_axis(): return jnp.sum(lax.all_to_all(own, far, 0, 0, tiled=True), axis=0)  42 us
    all_to_all x2, blocking collectives, summed_on_arrival(): lax.all_to_all(blocks, axis, split_axis=0, concat_axis=0, tiled=True)  22.3 us
    dot_general x1, matrix products, local(): jnp.dot(flat.reshape(-1, width), mixing, preferred_element_type=jnp.float32)  3.54 us
    reduce_sum x2, other arithmetic, summed_on_arrival(): return arrived.sum(axis=0)  2.34 us
    another operation x3, other arithmetic  2.33 us

commit v1 on v0

v1 whole, which is shorter than its diff:
```python
import math

import jax
import jax.numpy as jnp
from jax import lax
from jax.experimental import pallas as pl
from jax.experimental.pallas import tpu as pltpu
from jax.sharding import PartitionSpec as P

MESH = pl.DeviceIdType.MESH
ORDER = (2, 1, 3, 0)
SLOT = {k: i for i, k in enumerate(ORDER)}
NT = (((1,), (1,)), ((), ()))


def phase_weights(mom_ref, padded, weights):
    padded[...] = jnp.zeros_like(padded)
    padded[:, 0:125] = mom_ref[...]
    own = lax.broadcasted_iota(jnp.int32, (8, 128), 0)
    cos, sin = [], []
    for row, axis in enumerate(("gx", "gy", "gz")):
        turns = (padded[row : row + 1, :] * (own + 8 * lax.axis_index(axis))) & 63
        angle = turns.astype(jnp.float32) * (2.0 * math.pi / 64.0)
        cos.append(jnp.cos(angle))
        sin.append(jnp.sin(angle))
    cos_yz = jnp.concatenate([cos[1][y : y + 1] * cos[2] - sin[1][y : y + 1] * sin[2] for y in range(8)], axis=0)
    sin_yz = jnp.concatenate([sin[1][y : y + 1] * cos[2] + cos[1][y : y + 1] * sin[2] for y in range(8)], axis=0)
    for x in range(8):
        c = (cos[0][x : x + 1] * cos_yz - sin[0][x : x + 1] * sin_yz).astype(jnp.bfloat16)
        s = (sin[0][x : x + 1] * cos_yz + cos[0][x : x + 1] * sin_yz).astype(jnp.bfloat16)
        rows, more = pl.ds(64 * x, 64), pl.ds(512 + 64 * x, 64)
        weights[rows, 0:128] = c
        weights[rows, 128:256] = -s
        weights[more, 0:128] = s
        weights[more, 128:256] = c


def mixing_rows(src_ref, code_ref, core):
    raw = lax.broadcasted_iota(jnp.int32, (128, 64), 0)
    src, code = src_ref[...], code_ref[...]
    one, none = jnp.float32(1.0), jnp.float32(0.0)
    real_sign = jnp.where(code == 0, one, jnp.where(code == 2, -one, none))
    imag_sign = jnp.where(code == 1, one, jnp.where(code == 3, -one, none))
    from_real = jnp.where(raw == src, one, none)
    from_imag = jnp.where(raw == src + 64, one, none)
    to_real = from_real * real_sign - from_imag * imag_sign
    to_imag = from_real * imag_sign + from_imag * real_sign
    row = lax.broadcasted_iota(jnp.int32, (64, 64), 0)
    channel = lax.broadcasted_iota(jnp.int32, (64, 64), 1)
    outer, inner, last = (row >> 3) & 3, (row >> 1) & 3, row & 1
    side = (row >> 5) ^ core
    result = []
    for z, y in ((outer, inner), (inner, outer)):
        chosen = jnp.where(channel == z * 16 + y * 4 + side * 2 + last, one, none).astype(jnp.bfloat16)
        parts = [
            lax.dot_general(chosen, part.astype(jnp.bfloat16), NT, preferred_element_type=jnp.float32)
            for part in (to_real, to_imag)
        ]
        result.append(jnp.concatenate(parts, axis=0).astype(jnp.bfloat16))
    return result


def kernel(corr, mom_ref, src_ref, code_ref, out_ref, inbuf, padded, weights, left, own, give, take,
           z1, z1r, z2, z2r, y1, y1r, y2, y2r, a1, a1r, a2, a2r, b1, b1r, b2, b2r, p3, p3r,
           in_sem, core_send, core_recv, send_sem, recv_sem):
    gx, gy, gz = lax.axis_index("gx"), lax.axis_index("gy"), lax.axis_index("gz")
    x, y_hi, z, y_lo, core = gx // 2, gx % 2, gy, gz // 2, gz % 2
    y = y_hi * 4 + y_lo

    def at_x(k):
        return (((x + k) % 4) * 2 + y_hi, gy, gz)

    def at_y(k):
        to = (y + k) % 8
        return ((x * 2 + to // 4), gy, (to % 4) * 2 + core)

    def at_z(k):
        return (gx, (z + k) % 8, gz)

    partner = (gx, gy, y_lo * 2 + (1 - core))

    barrier = pltpu.get_barrier_semaphore()
    peers = [partner] + [at_x(k) for k in range(1, 4)]
    peers += [at_y(k) for k in range(1, 8)] + [at_z(k) for k in range(1, 8)]
    for peer in peers:
        pl.semaphore_signal(barrier, inc=1, device_id=peer, device_id_type=MESH)

    loads = []
    for i, k in enumerate(ORDER):
        rows = pl.ds(pl.multiple_of(((x + k) % 4) * 4096, 4096), 4096)
        load = pltpu.make_async_copy(corr.at[rows], inbuf.at[i], in_sem.at[i])
        load.start()
        loads.append(load)

    phase_weights(mom_ref, padded, weights)
    mix_zy, mix_yz = mixing_rows(src_ref, code_ref, core)

    sent = []

    def send(src, dst, channel, to):
        copy = pltpu.make_async_remote_copy(
            src_ref=src, dst_ref=dst, send_sem=send_sem.at[channel], recv_sem=recv_sem.at[channel],
            device_id=to, device_id_type=MESH)
        copy.start()

    def arrived(ref, channel):
        pltpu.make_async_copy(ref, ref, recv_sem.at[channel]).wait()

    def departed(ref, channel):
        pltpu.make_async_copy(ref, ref, send_sem.at[channel]).wait()

    swaps = []

    def compute(i):
        loads[i].wait()
        for t in range(8):
            mix = mix_zy if t % 4 in (0, 3) else mix_yz
            mixed = lax.dot_general(
                mix, inbuf[i, t * 512 : (t + 1) * 512, :], NT, preferred_element_type=jnp.float32
            ).astype(jnp.bfloat16)
            left[t * 64 : (t + 1) * 64, 0:512] = mixed[0:64]
            left[t * 64 : (t + 1) * 64, 512:1024] = mixed[64:128]
        product = jnp.dot(left[...], weights[...], preferred_element_type=jnp.float32)
        for t in range(8):
            for half in range(2):
                lanes = slice(half * 128, half * 128 + 128)
                own[i, t, half] = product[t * 64 : t * 64 + 32, lanes]
                give[i, t, half] = product[t * 64 + 32 : t * 64 + 64, lanes]
        if i == 0:
            pl.semaphore_wait(barrier, len(peers))
        swap = pltpu.make_async_remote_copy(
            src_ref=give.at[i], dst_ref=take.at[i], send_sem=core_send.at[i], recv_sem=core_recv.at[i],
            device_id=partner, device_id_type=MESH)
        swap.start()
        swaps.append(swap)

    def first_phase(i):
        swaps[i].wait_recv()
        for yh in range(2):
            for half in range(2):
                for tt in range(4):
                    t = yh * 4 + tt
                    value = (own[i, t, half] + take[i, t, half]).reshape(4, 8, 128)
                    if tt == 0:
                        for q in range(4):
                            z1[half * 4 + q, i, yh] = value[q]
                    elif tt == 1:
                        for q in range(4):
                            y1[yh * 4 + q, i, half] = value[q]
                    elif tt == 2:
                        for q in range(4):
                            a1[i, yh * 4 + q, half] = value[q]
                    else:
                        for q in range(4):
                            b1[i, half * 4 + q, yh] = value[q]
        k = ORDER[i]
        if k != 0:
            send(a1.at[i], a1r.at[k - 1], 0, at_x(k))
            send(b1.at[i], b1r.at[k - 1], 1, at_x(k))
        for k in (4, 3, 5, 2, 6, 1, 7):
            send(z1.at[(z + k) % 8, i], z1r.at[k - 1, i], 2, at_z(k))
            send(y1.at[(y + k) % 8, i], y1r.at[k - 1, i], 3, at_y(k))

    for i in range(4):
        compute(i)
        if i >= 1:
            first_phase(i - 1)
    first_phase(3)

    arrived(a1r, 0)
    a2[...] = a1[SLOT[0]] + a1r[0] + a1r[1] + a1r[2]
    for k in (4, 3, 5, 2, 6, 1, 7):
        send(a2.at[(y + k) % 8], a2r.at[k - 1], 4, at_y(k))
    arrived(b1r, 1)
    b2[...] = b1[SLOT[0]] + b1r[0] + b1r[1] + b1r[2]
    for k in (4, 3, 5, 2, 6, 1, 7):
        send(b2.at[(z + k) % 8], b2r.at[k - 1], 5, at_z(k))
    arrived(z1r, 2)
    z2[...] = z1[z] + ((z1r[0] + z1r[1]) + (z1r[2] + z1r[3])) + ((z1r[4] + z1r[5]) + z1r[6])
    for k in (2, 1, 3):
        send(z2.at[SLOT[k]], z2r.at[k - 1], 6, at_x(k))
    arrived(y1r, 3)
    y2[...] = y1[y] + ((y1r[0] + y1r[1]) + (y1r[2] + y1r[3])) + ((y1r[4] + y1r[5]) + y1r[6])
    for k in (2, 1, 3):
        send(y2.at[SLOT[k]], y2r.at[k - 1], 7, at_x(k))

    def spread(stream, value, at, mine):
        rows = value.reshape(16, 128)
        for q in range(8):
            p3[stream, q] = rows[2 * q : 2 * q + 2]
        for k in (4, 3, 5, 2, 6, 1, 7):
            send(p3.at[stream, (mine + k) % 8], p3r.at[stream, k - 1], 8 + stream, at(k))

    arrived(z2r, 6)
    spread(0, z2[SLOT[0]] + z2r[0] + z2r[1] + z2r[2], at_y, y)
    arrived(y2r, 7)
    spread(1, y2[SLOT[0]] + y2r[0] + y2r[1] + y2r[2], at_z, z)
    arrived(a2r, 4)
    spread(2, a2[y] + ((a2r[0] + a2r[1]) + (a2r[2] + a2r[3])) + ((a2r[4] + a2r[5]) + a2r[6]), at_z, z)
    arrived(b2r, 5)
    spread(3, b2[z] + ((b2r[0] + b2r[1]) + (b2r[2] + b2r[3])) + ((b2r[4] + b2r[5]) + b2r[6]), at_y, y)

    for stream, mine in enumerate((y, z, z, y)):
        arrived(p3r.at[stream], 8 + stream)
        total = p3[stream, mine]
        for k in range(7):
            total = total + p3r[stream, k]
        out_ref[stream] = total[:, 0:125] * (1.0 / 512.0)

    for swap in swaps:
        swap.wait_send()
    for channel, ref in enumerate((a1r, b1r, z1r, y1r, a2r, b2r, z2r, y2r)):
        departed(ref, channel)
    for stream in range(4):
        departed(p3r.at[stream], 8 + stream)


def local(correlators, momenta, source_channel, phase_code):
    f32, bf16 = jnp.float32, jnp.bfloat16
    vmem = pl.BlockSpec(memory_space=pltpu.VMEM)
    long = [(8, 4, 2, 8, 128), (7, 4, 2, 8, 128), (4, 2, 8, 128), (3, 2, 8, 128)]
    wide = [(4, 8, 2, 8, 128), (3, 8, 2, 8, 128), (8, 2, 8, 128), (7, 2, 8, 128)]
    scratch = [
        pltpu.VMEM((4, 4096, 128), bf16),
        pltpu.VMEM((3, 128), jnp.int32),
        pltpu.VMEM((1024, 256), bf16),
        pltpu.VMEM((512, 1024), bf16),
    ]
    scratch += [pltpu.VMEM((4, 8, 2, 32, 128), f32)] * 3
    scratch += [pltpu.VMEM(shape, f32) for shape in long + long + wide + wide]
    scratch += [pltpu.VMEM((4, 8, 2, 128), f32), pltpu.VMEM((4, 7, 2, 128), f32)]
    scratch += [pltpu.SemaphoreType.DMA((4,))] * 3 + [pltpu.SemaphoreType.DMA((12,))] * 2
    out = pl.pallas_call(
        kernel,
        out_shape=jax.ShapeDtypeStruct((4, 2, 125), f32),
        in_specs=[pl.BlockSpec(memory_space=pl.ANY), vmem, vmem, vmem],
        out_specs=vmem,
        scratch_shapes=scratch,
        compiler_params=pltpu.CompilerParams(collective_id=0, has_side_effects=True),
        name="project",
    )(
        correlators.reshape(-1, correlators.shape[-1]),
        momenta.T,
        source_channel.reshape(1, -1),
        phase_code.reshape(1, -1),
    )
    return jnp.transpose(out, (0, 2, 1))


def solution(mesh):
    return jax.shard_map(
        local,
        mesh=mesh,
        in_specs=(P(None, "gx", "gy", "gz", None), P(), P(), P()),
        out_specs=P("gx", None, ("gy", "gz")),
        check_vma=False,
    )
```

time: 81.9 us -> 36.5 us (0.45)
  the two profiles are of different devices: /device:TPU:16 before, /device:TPU:1 now
where the time goes in v1:
time: 36.5 us; the launch traced here: 36.4 us
  Pallas kernels  35.1 us (96%)
  local copies, waits for them, and re-layouts  1.28 us (4%)
    pallas_call x1, Pallas kernels, local(): pl.pallas_call(kernel, out_shape=jax.ShapeDtypeStruct((4, 2, 125), f32),...  35.1 us
    unnamed x1, local copies, waits for them, and re-layouts  1.28 us

profile of v1, /device:TPU:1, one launch (start us, length us, event | category | flops | bytes accessed | tf_op | source)
XLA Modules:
  0.0 36.4 jit_solution(4909694103178874337)
XLA Ops:
  0.0 35.1 %project.1 = f32[4,2,125]{2,1,0:T(2,128)} custom-call(bf16[16384,128]{1,0:T(8,128)(2,1)} %bitcast.5, s32[3,125]{1,0:T(4,128)} %bitcast.7, s32[1,64]{1,0:T(1,128)} %bitcast.8, s32[1,64]{1,0:T(1,128)} %bitcast.9), custom_call_target="tpu_custom_call" | custom-call | tf_op jit(solution)/shard_map/project/pallas_call | solution.py:233
  35.1 1.3 %copy.6 = f32[4,125,2]{1,2,0:T(2,128)} copy(f32[4,125,2]{1,2,0:T(2,128)} %bitcast.6) | data formatting | bytes 8000

commit v2 on v1

--- a/solution.py
+++ b/solution.py
@@ -60,9 +60,9 @@
     return result
 
 
-def kernel(corr, mom_ref, src_ref, code_ref, out_ref, inbuf, padded, weights, left, own, give, take,
+def kernel(corr, mom_hbm, src_hbm, code_hbm, out_ref, inbuf, mom_ref, src_ref, code_ref, padded, weights, left, own, give, take,
            z1, z1r, z2, z2r, y1, y1r, y2, y2r, a1, a1r, a2, a2r, b1, b1r, b2, b2r, p3, p3r,
-           in_sem, core_send, core_recv, send_sem, recv_sem):
+           in_sem, small_sem, core_send, core_recv, send_sem, recv_sem):
     gx, gy, gz = lax.axis_index("gx"), lax.axis_index("gy"), lax.axis_index("gz")
     x, y_hi, z, y_lo, core = gx // 2, gx % 2, gy, gz // 2, gz % 2
     y = y_hi * 4 + y_lo
@@ -91,6 +91,13 @@
         load = pltpu.make_async_copy(corr.at[rows], inbuf.at[i], in_sem.at[i])
         load.start()
         loads.append(load)
+    small = []
+    for i, (src, dst) in enumerate(((mom_hbm, mom_ref), (src_hbm, src_ref), (code_hbm, code_ref))):
+        load = pltpu.make_async_copy(src, dst, small_sem.at[i])
+        load.start()
+        small.append(load)
+    for load in small:
+        load.wait()
 
     phase_weights(mom_ref, padded, weights)
     mix_zy, mix_yz = mixing_rows(src_ref, code_ref, core)
@@ -217,11 +224,14 @@
 
 def local(correlators, momenta, source_channel, phase_code):
     f32, bf16 = jnp.float32, jnp.bfloat16
-    vmem = pl.BlockSpec(memory_space=pltpu.VMEM)
+    hbm = pl.BlockSpec(memory_space=pltpu.HBM)
     long = [(8, 4, 2, 8, 128), (7, 4, 2, 8, 128), (4, 2, 8, 128), (3, 2, 8, 128)]
     wide = [(4, 8, 2, 8, 128), (3, 8, 2, 8, 128), (8, 2, 8, 128), (7, 2, 8, 128)]
     scratch = [
         pltpu.VMEM((4, 4096, 128), bf16),
+        pltpu.VMEM((3, 125), jnp.int32),
+        pltpu.VMEM((1, 64), jnp.int32),
+        pltpu.VMEM((1, 64), jnp.int32),
         pltpu.VMEM((3, 128), jnp.int32),
         pltpu.VMEM((1024, 256), bf16),
         pltpu.VMEM((512, 1024), bf16),
@@ -229,20 +239,25 @@
     scratch += [pltpu.VMEM((4, 8, 2, 32, 128), f32)] * 3
     scratch += [pltpu.VMEM(shape, f32) for shape in long + long + wide + wide]
     scratch += [pltpu.VMEM((4, 8, 2, 128), f32), pltpu.VMEM((4, 7, 2, 128), f32)]
-    scratch += [pltpu.SemaphoreType.DMA((4,))] * 3 + [pltpu.SemaphoreType.DMA((12,))] * 2
+    scratch += [pltpu.SemaphoreType.DMA((4,)), pltpu.SemaphoreType.DMA((3,))] + [pltpu.SemaphoreType.DMA((4,))] * 2 + [pltpu.SemaphoreType.DMA((12,))] * 2
     out = pl.pallas_call(
         kernel,
         out_shape=jax.ShapeDtypeStruct((4, 2, 125), f32),
-        in_specs=[pl.BlockSpec(memory_space=pl.ANY), vmem, vmem, vmem],
-        out_specs=vmem,
+        in_specs=[hbm, hbm, hbm, hbm],
+        out_specs=pl.BlockSpec(memory_space=pltpu.VMEM),
         scratch_shapes=scratch,
-        compiler_params=pltpu.CompilerParams(collective_id=0, has_side_effects=True),
+        compiler_params=pltpu.CompilerParams(collective_id=0, has_side_effects=True, vmem_limit_bytes=24 * 1024 * 1024),
         name="project",
     )(
-        correlators.reshape(-1, correlators.shape[-1]),
-        momenta.T,
-        source_channel.reshape(1, -1),
-        phase_code.reshape(1, -1),
+        *(
+            pltpu.with_memory_space_constraint(value, pltpu.HBM)
+            for value in (
+                correlators.reshape(-1, correlators.shape[-1]),
+                momenta.T,
+                source_channel.reshape(1, -1),
+                phase_code.reshape(1, -1),
+            )
+        )
     )
     return jnp.transpose(out, (0, 2, 1))
 

time: 36.5 us -> 34.4 us (0.942)
  Pallas kernels: 35.1 us -> 33.7 us
  local copies, waits for them, and re-layouts: 1.28 us -> 0.6 us
    pallas_call x1, Pallas kernels: 35.1 us -> 33.7 us  [local(): pl.pallas_call(kernel, out_shape=jax.ShapeDtypeStruct((4, 2, 125), f32),...]
    unnamed x1, local copies, waits for them, and re-layouts: 1.28 us -> 0.6 us
where the time goes in v2:
time: 34.4 us; the launch traced here: 34.3 us
  Pallas kernels  33.7 us (98%)
  local copies, waits for them, and re-layouts  0.6 us (2%)
    pallas_call x1, Pallas kernels, local(): pl.pallas_call(kernel, out_shape=jax.ShapeDtypeStruct((4, 2, 125), f32),...  33.7 us

profile of v2, /device:TPU:1, one launch (start us, length us, event | category | flops | bytes accessed | tf_op | source)
XLA Modules:
  0.0 34.3 jit_solution(61812551237614645)
XLA Ops:
  0.0 33.7 %project.1 = f32[4,2,125]{2,1,0:T(2,128)S(1)} custom-call(bf16[16384,128]{1,0:T(8,128)(2,1)} %bitcast.6, s32[3,125]{1,0:T(4,128)} %bitcast.7, s32[1,64]{1,0:T(1,128)} %bitcast.8, s32[1,64]{1,0:T(1,128)} %bitcast.9), custom_call_target="tpu_custom_call" | custom-call | tf_op jit(solution)/shard_map/project/pallas_call | solution.py:243
  33.7 0.6 %copy.6 = f32[4,125,2]{1,2,0:T(2,128)} copy(f32[4,125,2]{1,2,0:T(2,128)S(1)} %bitcast.5) | data formatting | bytes 8000

commit v3 on v2

--- a/solution.py
+++ b/solution.py
@@ -10,6 +10,7 @@
 MESH = pl.DeviceIdType.MESH
 ORDER = (2, 1, 3, 0)
 SLOT = {k: i for i, k in enumerate(ORDER)}
+FAR_FIRST = (4, 3, 5, 2, 6, 1, 7)
 NT = (((1,), (1,)), ((), ()))
 
 
@@ -116,7 +117,7 @@
     def departed(ref, channel):
         pltpu.make_async_copy(ref, ref, send_sem.at[channel]).wait()
 
-    swaps = []
+    swaps = {}
 
     def compute(i):
         loads[i].wait()
@@ -131,42 +132,47 @@
         for t in range(8):
             for half in range(2):
                 lanes = slice(half * 128, half * 128 + 128)
-                own[i, t, half] = product[t * 64 : t * 64 + 32, lanes]
-                give[i, t, half] = product[t * 64 + 32 : t * 64 + 64, lanes]
+                at = (i, t % 4 // 2, t // 4 * 2 + t % 2, half)
+                own[at] = product[t * 64 : t * 64 + 32, lanes]
+                give[at] = product[t * 64 + 32 : t * 64 + 64, lanes]
         if i == 0:
             pl.semaphore_wait(barrier, len(peers))
-        swap = pltpu.make_async_remote_copy(
-            src_ref=give.at[i], dst_ref=take.at[i], send_sem=core_send.at[i], recv_sem=core_recv.at[i],
-            device_id=partner, device_id_type=MESH)
-        swap.start()
-        swaps.append(swap)
+        for part in (1, 0):
+            swap = pltpu.make_async_remote_copy(
+                src_ref=give.at[i, part], dst_ref=take.at[i, part], send_sem=core_send.at[2 * i + part],
+                recv_sem=core_recv.at[2 * i + part], device_id=partner, device_id_type=MESH)
+            swap.start()
+            swaps[i, part] = swap
 
     def first_phase(i):
-        swaps[i].wait_recv()
-        for yh in range(2):
-            for half in range(2):
-                for tt in range(4):
-                    t = yh * 4 + tt
-                    value = (own[i, t, half] + take[i, t, half]).reshape(4, 8, 128)
-                    if tt == 0:
-                        for q in range(4):
-                            z1[half * 4 + q, i, yh] = value[q]
-                    elif tt == 1:
-                        for q in range(4):
-                            y1[yh * 4 + q, i, half] = value[q]
-                    elif tt == 2:
-                        for q in range(4):
-                            a1[i, yh * 4 + q, half] = value[q]
-                    else:
-                        for q in range(4):
-                            b1[i, half * 4 + q, yh] = value[q]
+        def sums(part):
+            swaps[i, part].wait_recv()
+            for yh in range(2):
+                for half in range(2):
+                    for j in range(2):
+                        at = (i, part, yh * 2 + j, half)
+                        yield yh, half, j, (own[at] + take[at]).reshape(4, 8, 128)
+
+        for yh, half, j, value in sums(1):
+            for q in range(4):
+                if j == 0:
+                    a1[i, half, yh * 4 + q] = value[q]
+                else:
+                    b1[i, yh, half * 4 + q] = value[q]
         k = ORDER[i]
         if k != 0:
-            send(a1.at[i], a1r.at[k - 1], 0, at_x(k))
-            send(b1.at[i], b1r.at[k - 1], 1, at_x(k))
-        for k in (4, 3, 5, 2, 6, 1, 7):
-            send(z1.at[(z + k) % 8, i], z1r.at[k - 1, i], 2, at_z(k))
-            send(y1.at[(y + k) % 8, i], y1r.at[k - 1, i], 3, at_y(k))
+            for piece in range(2):
+                send(a1.at[i, piece], a1r.at[k - 1, piece], piece, at_x(k))
+                send(b1.at[i, piece], b1r.at[k - 1, piece], 2 + piece, at_x(k))
+        for yh, half, j, value in sums(0):
+            for q in range(4):
+                if j == 0:
+                    z1[half * 4 + q, i, yh] = value[q]
+                else:
+                    y1[yh * 4 + q, i, half] = value[q]
+        for k in FAR_FIRST:
+            send(z1.at[(z + k) % 8, i], z1r.at[k - 1, i], 4, at_z(k))
+            send(y1.at[(y + k) % 8, i], y1r.at[k - 1, i], 5, at_y(k))
 
     for i in range(4):
         compute(i)
@@ -174,59 +180,69 @@
             first_phase(i - 1)
     first_phase(3)
 
-    arrived(a1r, 0)
-    a2[...] = a1[SLOT[0]] + a1r[0] + a1r[1] + a1r[2]
-    for k in (4, 3, 5, 2, 6, 1, 7):
-        send(a2.at[(y + k) % 8], a2r.at[k - 1], 4, at_y(k))
-    arrived(b1r, 1)
-    b2[...] = b1[SLOT[0]] + b1r[0] + b1r[1] + b1r[2]
-    for k in (4, 3, 5, 2, 6, 1, 7):
-        send(b2.at[(z + k) % 8], b2r.at[k - 1], 5, at_z(k))
-    arrived(z1r, 2)
+    for piece in range(2):
+        arrived(a1r.at[:, piece], piece)
+        a2[piece] = a1[SLOT[0], piece] + a1r[0, piece] + a1r[1, piece] + a1r[2, piece]
+        for k in FAR_FIRST:
+            send(a2.at[piece, (y + k) % 8], a2r.at[piece, k - 1], 6, at_y(k))
+        arrived(b1r.at[:, piece], 2 + piece)
+        b2[piece] = b1[SLOT[0], piece] + b1r[0, piece] + b1r[1, piece] + b1r[2, piece]
+        for k in FAR_FIRST:
+            send(b2.at[piece, (z + k) % 8], b2r.at[piece, k - 1], 7, at_z(k))
+    arrived(z1r, 4)
     z2[...] = z1[z] + ((z1r[0] + z1r[1]) + (z1r[2] + z1r[3])) + ((z1r[4] + z1r[5]) + z1r[6])
     for k in (2, 1, 3):
-        send(z2.at[SLOT[k]], z2r.at[k - 1], 6, at_x(k))
-    arrived(y1r, 3)
+        send(z2.at[SLOT[k]], z2r.at[k - 1], 8, at_x(k))
+    arrived(y1r, 5)
     y2[...] = y1[y] + ((y1r[0] + y1r[1]) + (y1r[2] + y1r[3])) + ((y1r[4] + y1r[5]) + y1r[6])
     for k in (2, 1, 3):
-        send(y2.at[SLOT[k]], y2r.at[k - 1], 7, at_x(k))
+        send(y2.at[SLOT[k]], y2r.at[k - 1], 9, at_x(k))
 
     def spread(stream, value, at, mine):
         rows = value.reshape(16, 128)
         for q in range(8):
             p3[stream, q] = rows[2 * q : 2 * q + 2]
-        for k in (4, 3, 5, 2, 6, 1, 7):
-            send(p3.at[stream, (mine + k) % 8], p3r.at[stream, k - 1], 8 + stream, at(k))
-
-    arrived(z2r, 6)
+        for k in FAR_FIRST:
+            send(p3.at[stream, (mine + k) % 8], p3r.at[stream, k - 1], 10 + stream, at(k))
+
+    def all_of(mine, other):
+        total = mine
+        for k in range(7):
+            total = total + other[:, k]
+        return total
+
+    arrived(z2r, 8)
     spread(0, z2[SLOT[0]] + z2r[0] + z2r[1] + z2r[2], at_y, y)
-    arrived(y2r, 7)
+    arrived(y2r, 9)
     spread(1, y2[SLOT[0]] + y2r[0] + y2r[1] + y2r[2], at_z, z)
-    arrived(a2r, 4)
-    spread(2, a2[y] + ((a2r[0] + a2r[1]) + (a2r[2] + a2r[3])) + ((a2r[4] + a2r[5]) + a2r[6]), at_z, z)
-    arrived(b2r, 5)
-    spread(3, b2[z] + ((b2r[0] + b2r[1]) + (b2r[2] + b2r[3])) + ((b2r[4] + b2r[5]) + b2r[6]), at_y, y)
+    arrived(a2r, 6)
+    spread(2, all_of(a2[:, y], a2r), at_z, z)
+    arrived(b2r, 7)
+    spread(3, all_of(b2[:, z], b2r), at_y, y)
 
     for stream, mine in enumerate((y, z, z, y)):
-        arrived(p3r.at[stream], 8 + stream)
+        arrived(p3r.at[stream], 10 + stream)
         total = p3[stream, mine]
         for k in range(7):
             total = total + p3r[stream, k]
         out_ref[stream] = total[:, 0:125] * (1.0 / 512.0)
 
-    for swap in swaps:
+    for swap in swaps.values():
         swap.wait_send()
-    for channel, ref in enumerate((a1r, b1r, z1r, y1r, a2r, b2r, z2r, y2r)):
-        departed(ref, channel)
+    for piece in range(2):
+        departed(a1r.at[:, piece], piece)
+        departed(b1r.at[:, piece], 2 + piece)
+    for channel, ref in enumerate((z1r, y1r, a2r, b2r, z2r, y2r)):
+        departed(ref, 4 + channel)
     for stream in range(4):
-        departed(p3r.at[stream], 8 + stream)
+        departed(p3r.at[stream], 10 + stream)
 
 
 def local(correlators, momenta, source_channel, phase_code):
     f32, bf16 = jnp.float32, jnp.bfloat16
     hbm = pl.BlockSpec(memory_space=pltpu.HBM)
     long = [(8, 4, 2, 8, 128), (7, 4, 2, 8, 128), (4, 2, 8, 128), (3, 2, 8, 128)]
-    wide = [(4, 8, 2, 8, 128), (3, 8, 2, 8, 128), (8, 2, 8, 128), (7, 2, 8, 128)]
+    wide = [(4, 2, 8, 8, 128), (3, 2, 8, 8, 128), (2, 8, 8, 128), (2, 7, 8, 128)]
     scratch = [
         pltpu.VMEM((4, 4096, 128), bf16),
         pltpu.VMEM((3, 125), jnp.int32),
@@ -236,10 +252,10 @@
         pltpu.VMEM((1024, 256), bf16),
         pltpu.VMEM((512, 1024), bf16),
     ]
-    scratch += [pltpu.VMEM((4, 8, 2, 32, 128), f32)] * 3
+    scratch += [pltpu.VMEM((4, 2, 4, 2, 32, 128), f32)] * 3
     scratch += [pltpu.VMEM(shape, f32) for shape in long + long + wide + wide]
     scratch += [pltpu.VMEM((4, 8, 2, 128), f32), pltpu.VMEM((4, 7, 2, 128), f32)]
-    scratch += [pltpu.SemaphoreType.DMA((4,)), pltpu.SemaphoreType.DMA((3,))] + [pltpu.SemaphoreType.DMA((4,))] * 2 + [pltpu.SemaphoreType.DMA((12,))] * 2
+    scratch += [pltpu.SemaphoreType.DMA((4,)), pltpu.SemaphoreType.DMA((3,))] + [pltpu.SemaphoreType.DMA((8,))] * 2 + [pltpu.SemaphoreType.DMA((14,))] * 2
     out = pl.pallas_call(
         kernel,
         out_shape=jax.ShapeDtypeStruct((4, 2, 125), f32),

time: 34.4 us -> 34 us (0.988)
  Pallas kernels: 33.7 us -> 33.3 us
where the time goes in v3:
time: 34 us; the launch traced here: 33.9 us
  Pallas kernels  33.3 us (98%)
  local copies, waits for them, and re-layouts  0.6 us (2%)
    pallas_call x1, Pallas kernels, local(): pl.pallas_call(kernel, out_shape=jax.ShapeDtypeStruct((4, 2, 125), f32),...  33.3 us

profile of v3, /device:TPU:1, one launch (start us, length us, event | category | flops | bytes accessed | tf_op | source)
XLA Modules:
  0.0 33.9 jit_solution(10497678599112374889)
XLA Ops:
  0.0 33.3 %project.1 = f32[4,2,125]{2,1,0:T(2,128)S(1)} custom-call(bf16[16384,128]{1,0:T(8,128)(2,1)} %bitcast.6, s32[3,125]{1,0:T(4,128)} %bitcast.7, s32[1,64]{1,0:T(1,128)} %bitcast.8, s32[1,64]{1,0:T(1,128)} %bitcast.9), custom_call_target="tpu_custom_call" | custom-call | tf_op jit(solution)/shard_map/project/pallas_call | solution.py:259
  33.3 0.6 %copy.6 = f32[4,125,2]{1,2,0:T(2,128)} copy(f32[4,125,2]{1,2,0:T(2,128)S(1)} %bitcast.5) | data formatting | bytes 8000
